TPU v7x, 32 devices: a whole 2x2x4 slice. The times are simulated.
32 devices in a mesh: dp: 8 (over z, y), grp: 4 (over x, core).
Axes of the slice: x: 2, y: 2, z: 4, core: 2. Of those that a mesh axis runs over, the one named last changes fastest.
Arguments:
- quot_ids: int32 [4096, 2], P(('dp', 'grp')), may hold values from 0 to 127
- rem_ids: int32 [4096, 2], P(('dp', 'grp')), may hold values from 0 to 16383, as said below
- labels: int32 [4096], P(('dp', 'grp')), may hold values 0 or 1
- quot_table: bfloat16 [2, 128, 512], replicated, may hold values from -6 to 6
- rem_table: bfloat16 [2, 16384, 512], P(None, 'grp'), may hold values from -6 to 6
- w1: bfloat16 [1024, 512], replicated, may hold values from -0.1875 to 0.1875
- b1: float32 [512], replicated, may hold values from -3 to 3
- w2: bfloat16 [512], replicated, may hold values from -0.5 to 0.5
- b2: float32 [1], replicated, may hold values from -3 to 3
Outputs:
- losses: float32 [4096], P(('dp', 'grp'))
- grad_rem: float32 [2, 16384, 512], P(None, 'grp', 'dp')
- grad_quot: float32 [2, 128, 512], replicated
- grad_w1: float32 [1024, 512], replicated
- grad_b1: float32 [512], replicated
- grad_w2: float32 [512], replicated
- grad_b2: float32 [1], replicated
Inputs may be any that keep to these rules, and one draw needn't show every extreme that they name: `rem_ids`: in each aligned block of 128 samples and each feature, at most 64 remainder indices r share the same r // 4096, and exactly 64 do for some value of r // 4096.
All inputs are finite; a program needn't handle non-finite values. No bound on the sum of `labels` on one device may be relied on, other than what follows from the above.
Results may differ from a plain program's by a relative error of at most 0.0051.
Values may be sent and summed in bfloat16 or wider, within the bound.
No kernel may reach another device: no remote copies, remote signals or barrier semaphores. Data moves between devices by JAX's collectives and lax.ppermute only.
A program may use at most 128 MiB of HBM per device.

v0:
```python
import jax
import jax.numpy as jnp
from jax import lax
from jax.sharding import PartitionSpec as P


def scatter_rows(shard_grad, positions, values):
    for feature in range(shard_grad.shape[0]):
        shard_grad = shard_grad.at[feature, positions[:, feature]].add(
            values[:, feature].astype(jnp.float32), mode="drop"
        )
    return shard_grad


def pick_rows(rem_table, wanted, filled):
    pieces = []
    for feature in range(rem_table.shape[0]):
        picked = jnp.take(rem_table[feature], wanted[:, feature], axis=0)
        pieces.append(jnp.where(filled[:, feature : feature + 1], picked, jnp.zeros_like(picked)))
    return jnp.concatenate(pieces, axis=1)


def on_device(quot_ids, rem_ids, labels, quot_table, rem_table, w1, b1, w2, b2):
    features = rem_ids.shape[1]
    shard_rows = rem_table.shape[1]
    model_width = rem_table.shape[2]
    table_rows = quot_table.shape[1]
    owner_index = lax.axis_index("grp")
    gathered_ids = lax.all_gather(rem_ids, "grp", axis=0, tiled=True)
    local_rows = gathered_ids - owner_index * shard_rows
    inside = (local_rows >= 0) & (local_rows < shard_rows)
    safe_rows = jnp.clip(local_rows, 0, shard_rows - 1)
    partial_value = pick_rows(rem_table, safe_rows, inside).astype(jnp.float32)
    rem_rows = lax.psum_scatter(
        partial_value.astype(jnp.bfloat16), "grp", scatter_dimension=0, tiled=True
    )
    quot_parts = []
    onehots = []
    for feature in range(features):
        onehot = (
            quot_ids[:, feature][:, None] == jnp.arange(table_rows, dtype=jnp.int32)[None, :]
        ).astype(jnp.bfloat16)
        onehots.append(onehot)
        quot_parts.append(jnp.dot(onehot, quot_table[feature], preferred_element_type=jnp.float32))
    quot_rows = jnp.concatenate(quot_parts, axis=1)
    rem_float = rem_rows.astype(jnp.float32)
    joined = (quot_rows * rem_float).astype(jnp.bfloat16)
    preact = jnp.dot(joined, w1, preferred_element_type=jnp.float32) + b1
    hidden = jax.nn.silu(preact).astype(jnp.bfloat16)
    logits = jnp.dot(hidden, w2, preferred_element_type=jnp.float32) + b2[0]
    target = labels.astype(jnp.float32)
    losses = jax.nn.softplus(logits) - target * logits
    dlogits = jax.nn.sigmoid(logits) - target
    grad_b2 = jnp.sum(dlogits)[None]
    grad_w2 = jnp.dot(dlogits, hidden.astype(jnp.float32), precision=lax.Precision.HIGHEST)
    sigmoid_pre = jax.nn.sigmoid(preact)
    slopes = sigmoid_pre * (1.0 + preact * (1.0 - sigmoid_pre))
    dpreact = dlogits[:, None] * w2.astype(jnp.float32)[None, :] * slopes
    grad_b1 = jnp.sum(dpreact, axis=0)
    rounded = dpreact.astype(jnp.bfloat16)
    grad_w1 = jnp.dot(joined.T, rounded, preferred_element_type=jnp.float32)
    djoined = jnp.dot(rounded, w1.T, preferred_element_type=jnp.float32)
    rem_grads = (djoined * quot_rows).astype(jnp.bfloat16)
    quot_grads = djoined * rem_float
    quot_list = []
    for feature in range(features):
        quot_list.append(
            jnp.dot(
                onehots[feature].astype(jnp.float32).T,
                quot_grads[:, feature * model_width : (feature + 1) * model_width],
                precision=lax.Precision.HIGHEST,
            )
        )
    grad_quot = jnp.stack(quot_list, axis=0)
    grad_w1, grad_b1, grad_w2, grad_b2, grad_quot = lax.psum(
        (grad_w1, grad_b1, grad_w2, grad_b2, grad_quot), ("dp", "grp")
    )
    group_rows = lax.all_gather(rem_grads, "grp", axis=0, tiled=True)
    group_rows = group_rows.reshape(group_rows.shape[0], features, model_width)
    positions = jnp.where(inside, local_rows, shard_rows)
    received = lax.all_to_all(group_rows, "dp", split_axis=2, concat_axis=0, tiled=True)
    all_positions = lax.all_gather(positions, "dp", axis=0, tiled=True)
    shard_grad = jnp.zeros((features, shard_rows, received.shape[2]), jnp.float32)
    grad_rem = scatter_rows(shard_grad, all_positions, received)
    return (losses, grad_rem, grad_quot, grad_w1, grad_b1, grad_w2, grad_b2)


def solution(mesh):
    placed = (
        P(("dp", "grp"), None),
        P(("dp", "grp"), None),
        P(("dp", "grp")),
        P(),
        P(None, "grp", None),
        P(),
        P(),
        P(),
        P(),
    )
    return jax.shard_map(
        on_device,
        mesh=mesh,
        in_specs=placed,
        out_specs=(P(("dp", "grp")), P(None, "grp", "dp"), P(), P(), P(), P(), P()),
        check_vma=False,
    )
```

profile of v0, /device:TPU:0, one launch (start us, length us, event | category | flops | bytes accessed | tf_op | source)
XLA Modules:
  0.0 262.6 jit_solution(8166397708621926012)
XLA Ops:
  7.2 6.4 %all_gather.9 = s32[512,2]{0,1:T(2,128)S(1)} all-gather(s32[128,2]{0,1:T(2,128)} %param.12), channel_id=1, replica_groups=mesh['dp'=8,'grp'=4] {'grp'}, dimensions={0}, use_global_device_ids=true | all-gather | bytes 5120 | tf_op jit(solution)/shard_map/all_gather | solution.py:29
  13.7 5.7 %slice_bitcast_fusion.1 = (bf16[4096,512]{1,0:T(8,128)(2,1)}, bf16[4096,512]{1,0:T(8,128)(2,1)}) fusion(bf16[2,4096,512]{2,1,0:T(8,128)(2,1)} %param.15), kind=kLoop, calls=%fused_computation.5 | loop fusion | bytes 16777216 | tf_op jit(solution)/shard_map/squeeze | solution.py:18
  19.5 4.7 %gather_fusion.1 = bf16[512,512]{1,0:T(8,128)(2,1)S(1)} fusion(bf16[4096,512]{1,0:T(8,128)(2,1)} %get-tuple-element.43, s32[1024]{0:T(1024)S(1)} %pad_clamp_fusion), kind=kCustom, calls=%fused_computation.1.clone | custom fusion | bytes 1050624 | tf_op jit(solution)/shard_map/jit(_take)/gather | solution.py:18
  24.3 4.8 %gather_fusion = bf16[512,512]{1,0:T(8,128)(2,1)S(1)} fusion(bf16[4096,512]{1,0:T(8,128)(2,1)} %get-tuple-element.42, s32[1024]{0:T(1024)S(1)} %pad_clamp_fusion.1), kind=kCustom, calls=%fused_computation.clone | custom fusion | bytes 1050624 | tf_op jit(solution)/shard_map/jit(_take)/gather | solution.py:18
  29.1 0.6 select_select_fusion
  29.6 1.1 pad_maximum_fusion
  32.3 25.1 %reduce-scatter.2.cloned.1.call-done = bf16[128,1024]{1,0:T(8,128)(2,1)} async-done(((bf16[512,1024]{1,0:T(8,128)(2,1)}), bf16[128,1024]{1,0:T(8,128)(2,1)}) %reduce-scatter.2.cloned.1.call-update) | async-done | bytes 262160 | tf_op jit(solution)/shard_map/reduce_scatter | solution.py:34
  57.4 1.3 multiply_convert_fusion.1
  58.7 1.3 fusion.30
  60.0 2.2 convert_multiply_fusion
  62.2 32.3 %all_gather.10 = s32[4096,2]{0,1:T(2,128)} all-gather(s32[512,2]{0,1:T(2,128)S(1)} %get-tuple-element.50), channel_id=1, replica_groups=mesh['dp'=8,'grp'=4] {'dp'}, dimensions={0}, use_global_device_ids=true | all-gather | bytes 36864 | tf_op jit(solution)/shard_map/all_gather | solution.py:82
  94.5 1.8 reshape.29
  96.4 3.8 %copy.25 = bf16[512,2,512]{0,1,2:T(2,128)(2,1)} copy(bf16[512,2,512]{2,1,0:T(2,128)(2,1)S(1)} %reshape.29) | data formatting | bytes 2097152 | tf_op jit(solution)/shard_map/reshape | solution.py:79
  100.1 5.4 %all-to-all-start = ((bf16[512,2,512]{0,1,2:T(2,128)(2,1)}), bf16[512,2,512]{0,1,2:T(2,128)(2,1)S(1)}, u32[]{:S(2)}, u32[]{:S(2)}) async-start(bf16[512,2,512]{0,1,2:T(2,128)(2,1)} %copy.25), calls=%async_computation.1 | async-start | bytes 2097152 | tf_op jit(solution)/shard_map/all_to_all | solution.py:81
  105.6 0.9 compare_select_fusion.1
  106.8 0.6 broadcast_select_fusion
  107.4 1.0 convolution_bitcast_fusion
  108.5 1.0 convolution_bitcast_fusion.1
  109.5 0.8 pad_maximum_fusion.2
  110.3 2.8 %fusion.14 = f32[1024,512]{1,0:T(8,128)} fusion(bf16[128,1024]{1,0:T(8,128)(2,1)} %reduce-scatter.2.cloned.1.call-done, f32[128,512]{1,0:T(8,128)S(1)} %fusion.8, f32[128,512]{1,0:T(8,128)S(1)} %fusion.10, f32[128,512]{1,0:T(8,128)S(1)} %get-tuple-element.58, f32[512]{0:T(512)} %copy-done.2, f32[128]{0:T(128)} %copy-done.3), kind=kOutput, calls=%fused_computation.39 | convolution fusion | flops 135397376 | bytes 3148288 | tf_op jit(solution)/shard_map/dot_general | solution.py:61
  113.2 0.8 fusion.29
  114.0 0.8 fusion.25
  114.8 40.5 %all-reduce.2 = (f32[512]{0:T(512)}, f32[512]{0:T(512)}, f32[1]{0:T(128)}) all-reduce(f32[512]{0:T(512)S(1)} %fusion.29, f32[512]{0:T(512)S(1)} %bitcast.59, f32[1]{0:T(128)} %bitcast.19), channel_id=1, replica_groups=mesh['dp'=8,'grp'=4] {'dp','grp'}, use_global_device_ids=true, to_apply=%region_6.8 | all-reduce | flops 1025 | bytes 8200 | tf_op jit(solution)/shard_map/psum | solution.py:75
  155.6 1.2 fusion.4
  156.8 1.9 copy.28
  158.7 1.8 copy.29
  160.5 24.8 %scatter_custom_fusion = f32[8192,64]{1,0:T(8,128)} fusion(s32[4096]{0:T(1024)} %get-tuple-element.62, f32[4096,64]{1,0:T(8,128)} %copy.28, f32[]{:T(128)} %constant.3.clone.1), kind=kCustom, calls=%fused_computation.6 | custom fusion | flops 262144 | bytes 2097664
  185.4 24.2 %scatter_fusion = f32[8192,64]{1,0:T(8,128)} fusion(f32[8192,64]{1,0:T(8,128)} %scatter_custom_fusion, s32[4096]{0:T(1024)S(1)} %get-tuple-element.61, f32[4096,64]{1,0:T(8,128)S(1)} %copy.29), kind=kCustom, calls=%fused_computation.3 | custom fusion | flops 262144 | bytes 3162112
  209.6 3.8 %copy.31 = f32[2,4096,64]{1,2,0:T(8,128)} copy(f32[2,4096,64]{2,1,0:T(8,128)} %bitcast.52) | data formatting | bytes 4194304
  213.4 37.7 %all-reduce.6.cloned.1.call-done = (f32[2,128,512]{2,1,0:T(8,128)}, f32[1024,512]{1,0:T(8,128)}) async-done(((f32[2,128,512]{2,1,0:T(8,128)}, f32[1024,512]{1,0:T(8,128)}), (f32[2,128,512]{2,1,0:T(8,128)}, f32[1024,512]{1,0:T(8,128)})) %all-reduce.6.cloned.1.call-update) | async-done | bytes 2621456 | tf_op jit(solution)/shard_map/psum | solution.py:75
  251.1 1.9 copy.39
  253.0 3.1 %copy.40 = f32[1024,512]{1,0:T(8,128)} copy(f32[1024,512]{1,0:T(8,128)} %get-tuple-element.66) | data formatting | bytes 4194304
  (51 shorter events, 1.7 us)
Async XLA Ops:
  7.2 50.3 %copy-start = (bf16[1024,512]{1,0:T(8,128)(2,1)S(1)}, bf16[1024,512]{1,0:T(8,128)(2,1)}, u32[]{:S(2)}) copy-start(bf16[1024,512]{1,0:T(8,128)(2,1)} %param.16) | copy-start | bytes 3145732
  7.2 50.2 %reduce-scatter.2.cloned.1.call-start = ((), (), s32[]{:S(2)}) async-start(), calls=%async_computation.2 | async-start | bytes 1310720 | tf_op jit(solution)/shard_map/reduce_scatter | solution.py:34
  24.2 6.6 %copy-start.6 = (bf16[512]{0:T(512)(128)(2,1)S(1)}, bf16[512]{0:T(512)(128)(2,1)}, u32[]{:S(2)}) copy-start(bf16[512]{0:T(512)(128)(2,1)} %param.18) | copy-start | bytes 3076
  24.3 7.3 %copy-start.7 = (s32[128,2]{0,1:T(2,128)S(1)}, s32[128,2]{0,1:T(2,128)}, u32[]{:S(2)}) copy-start(s32[128,2]{0,1:T(2,128)} %param.11) | copy-start | bytes 3076
  24.3 7.3 %copy-start.1 = (bf16[2,128,512]{2,1,0:T(8,128)(2,1)S(1)}, bf16[2,128,512]{2,1,0:T(8,128)(2,1)}, u32[]{:S(2)}) copy-start(bf16[2,128,512]{2,1,0:T(8,128)(2,1)} %param.14) | copy-start | bytes 786436
  29.0 28.4 %copy-start.11 = (f32[512]{0:T(512)S(1)}, f32[512]{0:T(512)}, u32[]{:S(2)}) copy-start(f32[512]{0:T(512)} %param.17) | copy-start | bytes 6148
  29.1 29.7 %copy-start.8 = (s32[128]{0:T(128)S(1)}, s32[128]{0:T(128)}, u32[]{:S(2)}) copy-start(s32[128]{0:T(128)} %param.13) | copy-start | bytes 1540
  30.8 63.7 %all-gather.2.cloned.1.call-start = ((), (), s32[]{:S(2)}) async-start(), calls=%async_computation.3 | async-start | bytes 1310720 | tf_op jit(solution)/shard_map/all_gather | solution.py:78
  30.8 63.6 %copy-start.2 = (f32[512]{0:T(512)}, f32[512]{0:T(512)S(1)}, u32[]{:S(2)}) copy-start(f32[512]{0:T(512)S(1)} %convert_element_type.44) | copy-start | bytes 6148
  31.5 0.5 copy-start.5
  31.5 28.5 %copy-start.4 = (s32[128]{0:T(128)}, s32[128]{0:T(128)S(1)}, u32[]{:S(2)}) copy-start(s32[128]{0:T(128)S(1)} %get-tuple-element.55) | copy-start | bytes 1540
  60.0 34.5 %copy-start.3 = (f32[128]{0:T(128)}, f32[128]{0:T(128)S(1)}, u32[]{:S(2)}) copy-start(f32[128]{0:T(128)S(1)} %get-tuple-element.41) | copy-start | bytes 1540
  60.0 46.4 %copy-start.9 = (s32[2]{0:T(128)S(1)}, s32[2]{0:T(128)}, u32[]{:S(2)}) copy-start(s32[2]{0:T(128)} %constant.13) | copy-start | bytes 28
  60.0 46.6 %copy-start.10 = (s32[2]{0:T(128)S(1)}, s32[2]{0:T(128)}, u32[]{:S(2)}) copy-start(s32[2]{0:T(128)} %constant.28) | copy-start | bytes 28
  100.1 55.2 %all-to-all-start = ((bf16[512,2,512]{0,1,2:T(2,128)(2,1)}), bf16[512,2,512]{0,1,2:T(2,128)(2,1)S(1)}, u32[]{:S(2)}, u32[]{:S(2)}) async-start(bf16[512,2,512]{0,1,2:T(2,128)(2,1)} %copy.25), calls=%async_computation.1 | async-start | bytes 2097152 | tf_op jit(solution)/shard_map/all_to_all | solution.py:81
  105.5 145.6 %all-reduce.6.cloned.1.call-start = ((), (), s32[]{:S(2)}) async-start(), calls=%async_computation.4 | async-start | bytes 5242880 | tf_op jit(solution)/shard_map/psum | solution.py:75
Sparse Core Ops, SparseCore 0:
  30.9 26.4 reduce-scatter.1
  62.3 16.6 all-gather.1
  113.3 137.7 all-reduce.5
where the time goes:
time: 263 us
  blocking collectives  79.2 us (30%)
  waiting for transfers between devices  62.9 us (24%)
  other arithmetic  55.4 us (21%)
  local copies, waits for them, and re-layouts  33.9 us (13%)
  between operations  14.7 us (6%)
  matrix products  10.9 us (4%)
  starting transfers between devices  5.49 us (2%)
    unnamed x5, other arithmetic  50 us
    psum x1, blocking collectives, on_device(): lax.psum((grad_w1, grad_b1, grad_w2, grad_b2, grad_quot), ('dp', 'grp'))  40.5 us
    psum x1, waiting for transfers between devices, on_device(): lax.psum((grad_w1, grad_b1, grad_w2, grad_b2, grad_quot), ('dp', 'grp'))  37.7 us
    all_gather x1, blocking collectives, on_device(): all_positions = lax.all_gather(positions, 'dp', axis=0, tiled=True)  32.3 us
    reduce_scatter x1, waiting for transfers between devices, on_device(): lax.psum_scatter(partial_value.astype(jnp.bfloat16), 'grp', scatter_dimen...  25.1 us
    gather x2, local copies, waits for them, and re-layouts, pick_rows(): picked = jnp.take(rem_table[feature], wanted[:, feature], axis=0)  9.47 us
    unnamed x28, local copies, waits for them, and re-layouts  9.05 us
    all_gather x1, blocking collectives, on_device(): gathered_ids = lax.all_gather(rem_ids, 'grp', axis=0, tiled=True)  6.42 us
  transfers between devices with their start and end apart: 4, of which 2 were waited for; matrix products, arithmetic and copies ran while one was open for 26% of the time, Pallas kernels for 0%

commit v1 on v0

--- a/solution.py
+++ b/solution.py
@@ -1,7 +1,16 @@
+import functools
 import jax
 import jax.numpy as jnp
 from jax import lax
 from jax.sharding import PartitionSpec as P
+
+
+def draw_lanes(local_block, group_axis, axis_key):
+    after = lax.psum(lax.psum(local_block, group_axis), axis_name=axis_key)
+    return after
+
+
+carry_series_all_all = functools.partial(draw_lanes, group_axis="grp", axis_key="dp")
 
 
 def scatter_rows(shard_grad, positions, values):
@@ -72,8 +81,8 @@
             )
         )
     grad_quot = jnp.stack(quot_list, axis=0)
-    grad_w1, grad_b1, grad_w2, grad_b2, grad_quot = lax.psum(
-        (grad_w1, grad_b1, grad_w2, grad_b2, grad_quot), ("dp", "grp")
+    grad_w1, grad_b1, grad_w2, grad_b2, grad_quot = carry_series_all_all(
+        (grad_w1, grad_b1, grad_w2, grad_b2, grad_quot)
     )
     group_rows = lax.all_gather(rem_grads, "grp", axis=0, tiled=True)
     group_rows = group_rows.reshape(group_rows.shape[0], features, model_width)

time: 263 us -> 273 us (1.038)
  waiting for transfers between devices: 62.9 us -> 75.3 us
  blocking collectives: 79.2 us -> 83.1 us
  matrix products: 10.9 us -> 7.06 us
    all_gather x1, blocking collectives: 32.3 us -> 46.2 us  [on_device(): all_positions = lax.all_gather(positions, 'dp', axis=0, tiled=True)]
    all_gather x1, waiting for transfers between devices: 0.02 us -> 13.3 us  [on_device(): group_rows = lax.all_gather(rem_grads, 'grp', axis=0, tiled=True)]
    psum x1 -> x2, blocking collectives: 40.5 us -> 30.5 us  [draw_lanes(): after = lax.psum(lax.psum(local_block, group_axis), axis_name=axis_key)]
    psum x1 -> x2, waiting for transfers between devices: 37.7 us -> 36.4 us  [draw_lanes(): after = lax.psum(lax.psum(local_block, group_axis), axis_name=axis_key)]
    unnamed x28 -> x22, local copies, waits for them, and re-layouts: 9.05 us -> 8.86 us
  transfers between devices with their start and end apart: 4 -> 5, of which waited for: 2 -> 4; matrix products, arithmetic and copies ran while one was open for 26% -> 25% of each run, Pallas kernels for 0% -> 0%
where the time goes in v1:
time: 273 us
  blocking collectives  83.1 us (30%)
  waiting for transfers between devices  75.3 us (28%)
  other arithmetic  53.3 us (20%)
  local copies, waits for them, and re-layouts  33.7 us (12%)
  between operations  14.7 us (5%)
  matrix products  7.06 us (3%)
  starting transfers between devices  5.81 us (2%)
    unnamed x5, other arithmetic  49.4 us
    all_gather x1, blocking collectives, on_device(): all_positions = lax.all_gather(positions, 'dp', axis=0, tiled=True)  46.2 us
    psum x2, waiting for transfers between devices, draw_lanes(): after = lax.psum(lax.psum(local_block, group_axis), axis_name=axis_key)  36.4 us
    psum x2, blocking collectives, draw_lanes(): after = lax.psum(lax.psum(local_block, group_axis), axis_name=axis_key)  30.5 us
    reduce_scatter x1, waiting for transfers between devices, on_device(): lax.psum_scatter(partial_value.astype(jnp.bfloat16), 'grp', scatter_dimen...  25.4 us
    all_gather x1, waiting for transfers between devices, on_device(): group_rows = lax.all_gather(rem_grads, 'grp', axis=0, tiled=True)  13.3 us
    gather x2, local copies, waits for them, and re-layouts, pick_rows(): picked = jnp.take(rem_table[feature], wanted[:, feature], axis=0)  9.42 us
    unnamed x22, local copies, waits for them, and re-layouts  8.86 us
  transfers between devices with their start and end apart: 5, of which 4 were waited for; matrix products, arithmetic and copies ran while one was open for 25% of the time, Pallas kernels for 0%

profile of v1, /device:TPU:0, one launch (start us, length us, event | category | flops | bytes accessed | tf_op | source)
XLA Modules:
  0.0 272.9 jit_solution(6802329701022157155)
XLA Ops:
  7.2 6.4 %all_gather.9 = s32[512,2]{0,1:T(2,128)S(1)} all-gather(s32[128,2]{0,1:T(2,128)} %param.12), channel_id=1, replica_groups=mesh['dp'=8,'grp'=4] {'grp'}, dimensions={0}, use_global_device_ids=true | all-gather | bytes 5120 | tf_op jit(solution)/shard_map/all_gather | solution.py:38
  13.7 5.7 %slice_bitcast_fusion.1 = (bf16[4096,512]{1,0:T(8,128)(2,1)}, bf16[4096,512]{1,0:T(8,128)(2,1)}) fusion(bf16[2,4096,512]{2,1,0:T(8,128)(2,1)} %param.15), kind=kLoop, calls=%fused_computation.5 | loop fusion | bytes 16777216 | tf_op jit(solution)/shard_map/squeeze | solution.py:27
  19.5 4.7 %gather_fusion.1 = bf16[512,512]{1,0:T(8,128)(2,1)S(1)} fusion(bf16[4096,512]{1,0:T(8,128)(2,1)} %get-tuple-element.48, s32[1024]{0:T(1024)S(1)} %pad_clamp_fusion), kind=kCustom, calls=%fused_computation.1.clone | custom fusion | bytes 1050624 | tf_op jit(solution)/shard_map/jit(_take)/gather | solution.py:27
  24.3 4.7 %gather_fusion = bf16[512,512]{1,0:T(8,128)(2,1)S(1)} fusion(bf16[4096,512]{1,0:T(8,128)(2,1)} %get-tuple-element.47, s32[1024]{0:T(1024)S(1)} %pad_clamp_fusion.1), kind=kCustom, calls=%fused_computation.clone | custom fusion | bytes 1050624 | tf_op jit(solution)/shard_map/jit(_take)/gather | solution.py:27
  29.0 0.6 select_select_fusion
  29.6 1.1 pad_maximum_fusion
  31.7 0.2 fusion.10
  31.9 25.4 %reduce-scatter.2.cloned.1.call-done = bf16[128,1024]{1,0:T(8,128)(2,1)} async-done(((bf16[512,1024]{1,0:T(8,128)(2,1)}), bf16[128,1024]{1,0:T(8,128)(2,1)}) %reduce-scatter.2.cloned.1.call-update) | async-done | bytes 262160 | tf_op jit(solution)/shard_map/reduce_scatter | solution.py:43
  57.4 1.4 multiply_convert_fusion.1
  58.8 1.3 fusion.30
  60.1 1.2 convert_multiply_fusion
  61.3 0.4 convolution_bitcast_fusion
  61.7 0.4 convolution_bitcast_fusion.1
  62.1 0.8 pad_maximum_fusion.2
  62.9 1.9 fusion.14
  64.8 13.3 %all-gather.2.cloned.1.call-done = bf16[512,1024]{1,0:T(8,128)(2,1)} async-done(((bf16[128,1024]{1,0:T(8,128)(2,1)}), bf16[512,1024]{1,0:T(8,128)(2,1)}) %all-gather.2.cloned.1.call-update) | async-done | bytes 1048592 | tf_op jit(solution)/shard_map/all_gather | solution.py:87
  78.1 1.8 reshape.29
  80.0 3.8 %copy.25 = bf16[512,2,512]{0,1,2:T(2,128)(2,1)} copy(bf16[512,2,512]{2,1,0:T(2,128)(2,1)S(1)} %reshape.29) | data formatting | bytes 2097152 | tf_op jit(solution)/shard_map/reshape | solution.py:88
  83.8 5.6 %all-to-all-start = ((bf16[512,2,512]{0,1,2:T(2,128)(2,1)}), bf16[512,2,512]{0,1,2:T(2,128)(2,1)S(1)}, u32[]{:S(2)}, u32[]{:S(2)}) async-start(bf16[512,2,512]{0,1,2:T(2,128)(2,1)} %copy.25), calls=%async_computation.1 | async-start | bytes 2097152 | tf_op jit(solution)/shard_map/all_to_all | solution.py:90
  89.4 46.2 %all_gather.10 = s32[4096,2]{0,1:T(2,128)S(1)} all-gather(s32[512,2]{0,1:T(2,128)S(1)} %get-tuple-element.55), channel_id=1, replica_groups=mesh['dp'=8,'grp'=4] {'dp'}, dimensions={0}, use_global_device_ids=true | all-gather | bytes 36864 | tf_op jit(solution)/shard_map/all_gather | solution.py:91
  135.7 5.4 %all-reduce.11.cloned.1.call-done = (f32[2,128,512]{2,1,0:T(8,128)}, f32[1024,512]{1,0:T(8,128)}) async-done(((f32[2,128,512]{2,1,0:T(8,128)}, f32[1024,512]{1,0:T(8,128)}), (f32[2,128,512]{2,1,0:T(8,128)}, f32[1024,512]{1,0:T(8,128)})) %all-reduce.11.cloned.1.call-update) | async-done | bytes 2621456 | tf_op jit(solution)/shard_map/psum | solution.py:9
  141.8 6.5 %all-reduce.4 = (f32[512]{0:T(512)S(1)}, f32[512]{0:T(512)S(1)}, f32[1]{0:T(128)}) all-reduce(f32[512]{0:T(512)S(1)} %fusion.29, f32[512]{0:T(512)S(1)} %bitcast.59, f32[1]{0:T(128)} %bitcast.19), channel_id=1, replica_groups=mesh['dp'=8,'grp'=4] {'grp'}, use_global_device_ids=true, to_apply=%region_8.10 | all-reduce | flops 1025 | bytes 8200 | tf_op jit(solution)/shard_map/psum | solution.py:9
  148.4 23.9 %all-reduce.2 = (f32[512]{0:T(512)}, f32[512]{0:T(512)}, f32[1]{0:T(128)}) all-reduce(f32[512]{0:T(512)S(1)} %get-tuple-element.40, f32[512]{0:T(512)S(1)} %get-tuple-element.41, f32[1]{0:T(128)} %get-tuple-element.42), channel_id=1, replica_groups=mesh['dp'=8,'grp'=4] {'dp'}, use_global_device_ids=true, to_apply=%region_9.11 | all-reduce | flops 1025 | bytes 8200 | tf_op jit(solution)/shard_map/psum | solution.py:9
  172.6 1.2 fusion.4
  173.8 1.9 copy.28
  175.7 1.8 copy.29
  177.5 24.8 %scatter_custom_fusion = f32[8192,64]{1,0:T(8,128)} fusion(s32[4096]{0:T(1024)S(1)} %get-tuple-element.67, f32[4096,64]{1,0:T(8,128)} %copy.28, f32[]{:T(128)} %constant.3.clone.1), kind=kCustom, calls=%fused_computation.6 | custom fusion | flops 262144 | bytes 2097664
  202.3 24.2 %scatter_fusion = f32[8192,64]{1,0:T(8,128)} fusion(f32[8192,64]{1,0:T(8,128)} %scatter_custom_fusion, s32[4096]{0:T(1024)S(1)} %get-tuple-element.66, f32[4096,64]{1,0:T(8,128)S(1)} %copy.29), kind=kCustom, calls=%fused_computation.3 | custom fusion | flops 262144 | bytes 3162112
  226.6 3.9 %copy.31 = f32[2,4096,64]{1,2,0:T(8,128)} copy(f32[2,4096,64]{2,1,0:T(8,128)} %bitcast.52) | data formatting | bytes 4194304
  230.4 31.1 %all-reduce.9.cloned.1.call-done = (f32[2,128,512]{2,1,0:T(8,128)}, f32[1024,512]{1,0:T(8,128)}) async-done(((f32[2,128,512]{2,1,0:T(8,128)}, f32[1024,512]{1,0:T(8,128)}), (f32[2,128,512]{2,1,0:T(8,128)}, f32[1024,512]{1,0:T(8,128)})) %all-reduce.9.cloned.1.call-update) | async-done | bytes 2621456 | tf_op jit(solution)/shard_map/psum | solution.py:9
  261.5 1.9 copy.41
  263.3 3.1 %copy.42 = f32[1024,512]{1,0:T(8,128)} copy(f32[1024,512]{1,0:T(8,128)} %get-tuple-element.71) | data formatting | bytes 4194304
  (49 shorter events, 1.6 us)
Async XLA Ops:
  7.2 50.2 %copy-start = (bf16[1024,512]{1,0:T(8,128)(2,1)S(1)}, bf16[1024,512]{1,0:T(8,128)(2,1)}, u32[]{:S(2)}) copy-start(bf16[1024,512]{1,0:T(8,128)(2,1)} %param.16) | copy-start | bytes 3145732
  7.2 50.2 %reduce-scatter.2.cloned.1.call-start = ((), (), s32[]{:S(2)}) async-start(), calls=%async_computation.2 | async-start | bytes 1310720 | tf_op jit(solution)/shard_map/reduce_scatter | solution.py:43
  29.6 1.2 copy-start.3
  29.6 1.9 copy-start.4
  29.6 1.9 copy-start.2
  29.6 27.8 %copy-start.8 = (f32[512]{0:T(512)S(1)}, f32[512]{0:T(512)}, u32[]{:S(2)}) copy-start(f32[512]{0:T(512)} %param.17) | copy-start | bytes 6148
  30.7 28.1 %copy-start.5 = (s32[128]{0:T(128)S(1)}, s32[128]{0:T(128)}, u32[]{:S(2)}) copy-start(s32[128]{0:T(128)} %param.13) | copy-start | bytes 1540
  30.7 47.4 %all-gather.2.cloned.1.call-start = ((), (), s32[]{:S(2)}) async-start(), calls=%async_computation.3 | async-start | bytes 1310720 | tf_op jit(solution)/shard_map/all_gather | solution.py:87
  57.4 2.7 copy-start.1
  61.3 79.8 %all-reduce.11.cloned.1.call-start = ((), (), s32[]{:S(2)}) async-start(), calls=%async_computation.5 | async-start | bytes 5242880 | tf_op jit(solution)/shard_map/psum | solution.py:9
  83.8 57.4 %copy-start.6 = (s32[2]{0:T(128)S(1)}, s32[2]{0:T(128)}, u32[]{:S(2)}) copy-start(s32[2]{0:T(128)} %constant.13) | copy-start | bytes 28
  83.8 57.6 %copy-start.7 = (s32[2]{0:T(128)S(1)}, s32[2]{0:T(128)}, u32[]{:S(2)}) copy-start(s32[2]{0:T(128)} %constant.28) | copy-start | bytes 28
  83.8 88.6 %all-to-all-start = ((bf16[512,2,512]{0,1,2:T(2,128)(2,1)}), bf16[512,2,512]{0,1,2:T(2,128)(2,1)S(1)}, u32[]{:S(2)}, u32[]{:S(2)}) async-start(bf16[512,2,512]{0,1,2:T(2,128)(2,1)} %copy.25), calls=%async_computation.1 | async-start | bytes 2097152 | tf_op jit(solution)/shard_map/all_to_all | solution.py:90
  89.4 172.1 %all-reduce.9.cloned.1.call-start = ((), (), s32[]{:S(2)}) async-start(), calls=%async_computation.4 | async-start | bytes 5242880 | tf_op jit(solution)/shard_map/psum | solution.py:9
Sparse Core Ops, SparseCore 0:
  30.8 26.4 reduce-scatter.1
  61.4 16.6 all-gather.1
  81.1 59.9 all-reduce.10
  144.7 116.6 all-reduce.8
